TPU v7x, 32 devices: a whole 2x2x4 slice. The times are simulated.
32 devices in a mesh: dp: 16 (over z, x, core), mp: 2 (over y).
Axes of the slice: x: 2, y: 2, z: 4, core: 2. Of those that a mesh axis runs over, the one named last changes fastest.
Arguments:
- context: bfloat16 [5120, 2048], P('dp', 'mp'), may hold values from -6 to 6
- out_weight: bfloat16 [2048, 3584], P('mp'), may hold values from -0.125 to 0.125
- cotangent: bfloat16 [5120, 3584], P('dp'), may hold values from -0.059814453 to 0.059814453
- norm_gain: float32 [3584], replicated, may hold values from 0.5 to 1.5
- first_moment: float32 [2, 1024, 3584], P('mp', 'dp'), may hold values from -6 to 6
- second_moment: float32 [2, 1024, 3584], P('mp', 'dp'), may hold values from 0.01 to 1
Outputs:
- new_weight: bfloat16 [2, 1024, 3584], P('mp', 'dp')
- new_first: float32 [2, 1024, 3584], P('mp', 'dp')
- new_second: float32 [2, 1024, 3584], P('mp', 'dp')
- grad_gain: float32 [3584], replicated
- grad_context: bfloat16 [5120, 2048], P('dp', 'mp')
All inputs are finite; a program needn't handle non-finite values.
Results may differ from a plain program's by a relative error of at most 0.005.
Values may be sent and summed in bfloat16 or wider, within the bound.
A program may use at most 128 MiB of HBM per device.

v0:
```python
import jax
import jax.numpy as jnp
from jax import lax
from jax.sharding import PartitionSpec as P

norm_floor = 0.1
learn_rate = 0.01
beta_one = 0.9
beta_two = 0.95
adam_floor = 1e-08


def adam_update(master, first_moment, second_moment, grad_shard):
    new_first = beta_one * first_moment + (1.0 - beta_one) * grad_shard
    new_second = beta_two * second_moment + (1.0 - beta_two) * grad_shard * grad_shard
    new_weight = (master - learn_rate * new_first / (jnp.sqrt(new_second) + adam_floor)).astype(
        jnp.bfloat16
    )
    return (new_weight, new_first, new_second)


def per_device(context, out_weight, cotangent, norm_gain, first_moment, second_moment):
    width = out_weight.shape[1]
    partial_value = jnp.dot(context, out_weight, preferred_element_type=jnp.float32)
    half_width = width // lax.axis_size("mp")
    offset = lax.axis_index("mp") * half_width
    attn_half = lax.psum_scatter(partial_value, "mp", scatter_dimension=1, tiled=True)
    gain_half = lax.dynamic_slice_in_dim(norm_gain, offset, half_width, 0)
    upstream = lax.dynamic_slice_in_dim(cotangent, offset, half_width, 1).astype(jnp.float32)
    squares = jnp.sum(attn_half * attn_half, axis=-1, keepdims=True)
    total_sq = lax.psum(squares, "mp")
    inverse = lax.rsqrt(total_sq / width + norm_floor)
    normed = attn_half * inverse
    scaled = upstream * gain_half
    product_half = jnp.sum(scaled * normed, axis=-1, keepdims=True)
    product_all = lax.psum(product_half, "mp")
    grad_half = (inverse * (scaled - normed * (product_all / width))).astype(jnp.bfloat16)
    grad_attn = lax.all_gather(grad_half, "mp", axis=1, tiled=True)
    gain_part = jnp.sum(upstream * normed, axis=0)
    gain_total = lax.psum(gain_part, "dp")
    grad_gain = lax.all_gather(gain_total, "mp", axis=0, tiled=True)
    shard_rows = first_moment.shape[1]
    master = lax.dynamic_slice_in_dim(
        out_weight, lax.axis_index("dp") * shard_rows, shard_rows, 0
    ).astype(jnp.float32)[None]
    grad_shard = lax.psum_scatter(
        lax.dot_general(
            context, grad_attn, (((0,), (0,)), ((), ())), preferred_element_type=jnp.float32
        ),
        "dp",
        scatter_dimension=0,
        tiled=True,
    )
    grad_context = lax.dot_general(
        grad_attn, out_weight, (((1,), (1,)), ((), ())), preferred_element_type=jnp.float32
    ).astype(jnp.bfloat16)
    new_weight, new_first, new_second = adam_update(
        master, first_moment, second_moment, grad_shard[None]
    )
    return (new_weight, new_first, new_second, grad_gain, grad_context)


def solution(mesh):
    return jax.shard_map(
        per_device,
        mesh=mesh,
        in_specs=(
            P("dp", "mp"),
            P("mp", None),
            P("dp", None),
            P(),
            P("mp", "dp", None),
            P("mp", "dp", None),
        ),
        out_specs=(
            P("mp", "dp", None),
            P("mp", "dp", None),
            P("mp", "dp", None),
            P(),
            P("dp", "mp"),
        ),
        check_vma=False,
    )
```

profile of v0, /device:TPU:0, one launch (start us, length us, event | category | flops | bytes accessed | tf_op | source)
XLA Modules:
  0.0 323.5 jit_solution(9615545915211681465)
XLA Ops:
  7.2 0.0 copy-start
  7.2 0.0 reduce-scatter.5.cloned.1.call-start
  7.2 1.0 copy-done
  8.3 7.7 %fusion.10 = f32[320,3584]{1,0:T(8,128)} fusion(bf16[320,1024]{1,0:T(8,128)(2,1)S(1)} %copy-done, bf16[1024,3584]{1,0:T(8,128)(2,1)} %param.7), kind=kOutput, calls=%fused_computation.20 | convolution fusion | flops 2348810240 | bytes 12582912 | tf_op jit(solution)/shard_map/dot_general | solution.py:24
  15.9 0.0 copy-start.5
  15.9 0.0 reduce-scatter.5.cloned.1.call-update
  16.0 0.0 all-gather.3.cloned.1.call-start
  16.0 0.6 copy-done.5
  16.6 0.1 dynamic_slice.11
  16.7 60.8 %reduce-scatter.5.cloned.1.call-done = f32[320,1792]{1,0:T(8,128)} async-done(((f32[320,3584]{1,0:T(8,128)}), f32[320,1792]{1,0:T(8,128)}) %reduce-scatter.5.cloned.1.call-update) | async-done | bytes 2293776 | tf_op jit(solution)/shard_map/reduce_scatter | solution.py:27
  77.5 0.0 copy-start.2
  77.5 2.0 multiply_reduce_fusion
  79.5 4.9 %psum.21 = f32[320,1]{0,1:T(1,128)S(1)} all-reduce(f32[320,1]{0,1:T(1,128)S(1)} %broadcast_in_dim.16), channel_id=1, replica_groups=mesh['dp'=16,'mp'=2] {'mp'}, use_global_device_ids=true, to_apply=%region_2.0 | all-reduce | flops 320 | bytes 2560 | tf_op jit(solution)/shard_map/psum | solution.py:31
  84.5 0.0 copy-done.2
  84.5 2.1 fusion.5
  86.6 4.9 %psum.22 = f32[320,1]{0,1:T(1,128)S(1)} all-reduce(f32[320,1]{0,1:T(1,128)S(1)} %broadcast_in_dim.17), channel_id=1, replica_groups=mesh['dp'=16,'mp'=2] {'mp'}, use_global_device_ids=true, to_apply=%region_4.0 | all-reduce | flops 320 | bytes 2560 | tf_op jit(solution)/shard_map/psum | solution.py:36
  91.5 2.8 fusion.4
  94.3 0.0 all-gather.3.cloned.1.call-update
  94.4 0.0 reduce-scatter.7.cloned.1.call-start
  94.4 35.4 %all-gather.3.cloned.1.call-done = bf16[320,3584]{1,0:T(8,128)(2,1)} async-done(((bf16[320,1792]{1,0:T(8,128)(2,1)}), bf16[320,3584]{1,0:T(8,128)(2,1)}) %all-gather.3.cloned.1.call-update) | async-done | bytes 2293776 | tf_op jit(solution)/shard_map/all_gather | solution.py:38
  129.8 8.9 %convolution_bitcast_fusion = f32[1024,3584]{0,1:T(8,128)} fusion(bf16[320,3584]{1,0:T(8,128)(2,1)} %all-gather.3.cloned.1.call-done, bf16[320,1024]{1,0:T(8,128)(2,1)S(1)} %copy-done), kind=kOutput, calls=%fused_computation | convolution fusion | flops 2348810240 | bytes 17629184 | tf_op jit(solution)/shard_map/dot_general | solution.py:47
  138.8 14.3 %copy.29 = f32[1024,3584]{1,0:T(8,128)} copy(f32[1024,3584]{0,1:T(8,128)} %convolution_bitcast_fusion) | data formatting | bytes 29360128
  153.1 0.0 reduce-scatter.7.cloned.1.call-update
  153.1 1.1 constant_dynamic-slice_fusion
  154.2 0.4 copy.31
  154.6 1.7 copy.24
  156.4 3.0 copy.25
  159.3 33.6 %psum.23 = f32[1792]{0:T(1024)S(1)} all-reduce(f32[1792]{0:T(1024)S(1)} %get-tuple-element.20), channel_id=1, replica_groups=mesh['dp'=16,'mp'=2] {'dp'}, use_global_device_ids=true, to_apply=%region_7.0 | all-reduce | flops 1792 | bytes 14336 | tf_op jit(solution)/shard_map/psum | solution.py:40
  192.9 4.4 %all-gather = f32[2,1,1792]{2,1,0:T(1,128)S(1)} all-gather(f32[1,1,1792]{2,1,0:T(1,128)S(1)} %reshape.15), channel_id=1, replica_groups=mesh['dp'=16,'mp'=2] {'mp'}, dimensions={0}, use_global_device_ids=true | all-gather | bytes 21504 | tf_op jit(solution)/shard_map/all_gather | solution.py:41
  197.4 0.6 reshape.16
  198.0 7.3 %convolution_convert_fusion = bf16[320,1024]{1,0:T(8,128)(2,1)} fusion(bf16[320,3584]{1,0:T(8,128)(2,1)} %all-gather.3.cloned.1.call-done, bf16[1024,3584]{1,0:T(8,128)(2,1)} %param.7), kind=kOutput, calls=%fused_computation.16 | convolution fusion | flops 2349137920 | bytes 10289152 | tf_op jit(solution)/shard_map/dot_general | solution.py:54
  205.3 98.2 %reduce-scatter.7.cloned.1.call-done = f32[64,3584]{1,0:T(8,128)} async-done(((f32[1024,3584]{1,0:T(8,128)}), f32[64,3584]{1,0:T(8,128)}) %reduce-scatter.7.cloned.1.call-update) | async-done | bytes 917520
  303.4 3.0 copy.30
  306.4 4.9 %fusion.8 = (bf16[1,64,3584]{1,2,0:T(8,128)(2,1)}, f32[1,64,3584]{1,2,0:T(8,128)}, f32[1,64,3584]{1,2,0:T(8,128)}) fusion(bf16[64,3584]{0,1:T(8,128)(2,1)S(1)} %copy.31, f32[64,3584]{0,1:T(8,128)} %copy.30, f32[1,64,3584]{1,2,0:T(8,128)S(1)} %copy.24, f32[1,64,3584]{1,2,0:T(8,128)} %copy.25), kind=kLoop, calls=%fused_computation.14 | loop fusion | flops 2981888 | bytes 5505024 | tf_op jit(solution)/shard_map/convert_element_type | solution.py:16
  311.3 0.0 copy-start.3
  311.3 0.0 copy-start.4
  311.3 0.0 copy-start.1
  311.3 3.1 copy.27
  314.4 0.0 copy-done.3
  314.4 1.4 copy.28
  315.9 0.0 copy-done.4
  315.9 1.1 copy.26
  316.9 0.0 copy-done.1
  (6 shorter events, 0.1 us)
Async XLA Ops:
  7.2 1.1 copy-start
  7.2 70.3 %reduce-scatter.5.cloned.1.call-start = ((), (), s32[]{:S(2)}) async-start(), calls=%async_computation.2 | async-start | bytes 6881280 | tf_op jit(solution)/shard_map/reduce_scatter | solution.py:27
  15.9 0.7 copy-start.5
  16.0 113.9 %all-gather.3.cloned.1.call-start = ((), (), s32[]{:S(2)}) async-start(), calls=%async_computation.3 | async-start | bytes 3440640 | tf_op jit(solution)/shard_map/all_gather | solution.py:38
  77.5 7.0 %copy-start.2 = (f32[320,1792]{1,0:T(8,128)S(1)}, f32[320,1792]{1,0:T(8,128)}, u32[]{:S(2)}) copy-start(f32[320,1792]{1,0:T(8,128)} %reduce-scatter.5.cloned.1.call-done) | copy-start | bytes 6881284
  94.4 209.1 %reduce-scatter.7.cloned.1.call-start = ((), (), s32[]{:S(2)}) async-start(), calls=%async_computation.4 | async-start | bytes 15597568
  311.3 3.1 copy-start.3
  311.3 4.5 %copy-start.4 = (bf16[1,64,3584]{1,2,0:T(8,128)(2,1)S(1)}, bf16[1,64,3584]{1,2,0:T(8,128)(2,1)}, u32[]{:S(2)}) copy-start(bf16[1,64,3584]{1,2,0:T(8,128)(2,1)} %get-tuple-element.22) | copy-start | bytes 1376260
  311.3 5.6 %copy-start.1 = (bf16[320,1024]{1,0:T(8,128)(2,1)S(1)}, bf16[320,1024]{1,0:T(8,128)(2,1)}, u32[]{:S(2)}) copy-start(bf16[320,1024]{1,0:T(8,128)(2,1)} %param.6) | copy-start | bytes 1966084
Sparse Core Ops, SparseCore 0:
  16.1 61.3 reduce-scatter.4
  94.5 35.3 all-gather.2
  153.3 150.1 reduce-scatter.6
where the time goes:
time: 324 us; the launch traced here: 323 us
  waiting for transfers between devices  194 us (60%)
  blocking collectives  47.8 us (15%)
  local copies, waits for them, and re-layouts  31.5 us (10%)
  matrix products  23.9 us (7%)
  between operations  13.8 us (4%)
  other arithmetic  11.9 us (4%)
    unnamed x4, waiting for transfers between devices  98.2 us
    reduce_scatter x1, waiting for transfers between devices, per_device(): lax.psum_scatter(partial_value, 'mp', scatter_dimension=1, tiled=True)  60.8 us
    all_gather x1, waiting for transfers between devices, per_device(): grad_attn = lax.all_gather(grad_half, 'mp', axis=1, tiled=True)  35.4 us
    psum x1, blocking collectives, per_device(): gain_total = lax.psum(gain_part, 'dp')  33.6 us
    unnamed x22, local copies, waits for them, and re-layouts  30.3 us
    dot_general x1, matrix products, per_device(): lax.dot_general(context, grad_attn, (((0,), (0,)), ((), ())), preferred_e...  8.95 us
    dot_general x1, matrix products, per_device(): jnp.dot(context, out_weight, preferred_element_type=jnp.float32)  7.67 us
    dot_general x1, matrix products, per_device(): lax.dot_general(grad_attn, out_weight, (((1,), (1,)), ((), ())), preferre...  7.26 us
  transfers between devices with their start and end apart: 3, of which 3 were waited for; matrix products, arithmetic and copies ran while one was open for 4% of the time, Pallas kernels for 0%

commit v1 on v0

v1 whole, which is shorter than its diff:
```python
import functools

import jax
import jax.numpy as jnp
from jax import lax
from jax.experimental import pallas as pl
from jax.experimental.pallas import tpu as pltpu
from jax.sharding import PartitionSpec as P

norm_floor = 0.1
learn_rate = 0.01
beta_one = 0.9
beta_two = 0.95
adam_floor = 1e-08

MESH = pl.DeviceIdType.MESH
F32 = jnp.float32
BF16 = jnp.bfloat16
LAG = 2


def kernel(
    cfg,
    ctx_hbm, w_hbm, cot_hbm, gain_hbm, m1_hbm, m2_hbm,
    nw_hbm, n1_hbm, n2_hbm, gg_hbm, gc_hbm,
    wv, ctx, ctxt_all, ctxt, cot, gain, psend, precv, own, stat_s, stat_r, g,
    sends, recvs, keeps, m1, m2, master, nw, gc_acc, gc_out,
    gp, gpr, gfin,
    in_sem, w_sem, cot_sem, m_sem, out_sem, gc_sem, gg_sem,
    ps_s, ps_r, st_s, st_r, cx_s, cx_r, gy_s, gy_r, gm_s, gm_r,
    rs_s, rs_r, gg_s, gg_r,
):
    n, bits, half, chunks, cw, rows, tok, heads, width = cfg
    dp, mp = lax.axis_index("dp"), lax.axis_index("mp")
    peer = 1 - mp

    def flip(index, bit):
        return index + (1 << bit) * (1 - 2 * ((index // (1 << bit)) % 2))

    def peer_id():
        return (dp, peer)

    def bit_id(bit):
        return (flip(dp, bit), mp)

    def column(r):
        first = jnp.where(r < half, mp * half + r, peer * half + r - half)
        return pl.multiple_of(first * cw, cw)

    def ctx_copy():
        return pltpu.make_async_copy(ctx_hbm, ctx.at[pl.ds(0, tok)], in_sem.at[0])

    def gain_copy():
        return pltpu.make_async_copy(gain_hbm.at[pl.ds(mp * half, half)], gain, in_sem.at[1])

    def w_copy(r):
        return pltpu.make_async_copy(w_hbm.at[:, pl.ds(column(r), cw)], wv.at[r], w_sem.at[r])

    def cot_copy(r):
        return pltpu.make_async_copy(cot_hbm.at[:, pl.ds(column(r), cw)], cot.at[r], cot_sem.at[r])

    def m_copies(r):
        cols = pl.ds(column(r), cw)
        return (
            pltpu.make_async_copy(m1_hbm.at[0, :, cols], m1.at[r], m_sem.at[0, r]),
            pltpu.make_async_copy(m2_hbm.at[0, :, cols], m2.at[r], m_sem.at[1, r]),
            pltpu.make_async_copy(
                w_hbm.at[pl.ds(pl.multiple_of(dp * rows, rows), rows), cols], master.at[r], m_sem.at[2, r]
            ),
        )

    def out_copies(r):
        cols = pl.ds(column(r), cw)
        return (
            pltpu.make_async_copy(nw.at[r], nw_hbm.at[0, :, cols], out_sem.at[0, r]),
            pltpu.make_async_copy(m1.at[r], n1_hbm.at[0, :, cols], out_sem.at[1, r]),
            pltpu.make_async_copy(m2.at[r], n2_hbm.at[0, :, cols], out_sem.at[2, r]),
        )

    def remote(src, dst, send_sem, recv_sem, device):
        return pltpu.make_async_remote_copy(
            src_ref=src, dst_ref=dst, send_sem=send_sem, recv_sem=recv_sem,
            device_id=device, device_id_type=MESH,
        )

    def partial_send(c):
        return remote(psend.at[c], precv.at[c], ps_s.at[c], ps_r.at[c], peer_id())

    def stat_send():
        return remote(stat_s, stat_r, st_s, st_r, peer_id())

    def ctx_send():
        return remote(ctx.at[pl.ds(0, tok)], ctx.at[pl.ds(tok, tok)], cx_s, cx_r, bit_id(0))

    def grad_peer(c):
        return remote(
            g.at[c, pl.ds(0, tok)], g.at[half + c, pl.ds(0, tok)], gy_s.at[c], gy_r.at[c], peer_id()
        )

    def grad_mate(r):
        return remote(
            g.at[r, pl.ds(0, tok)], g.at[r, pl.ds(tok, tok)], gm_s.at[r], gm_r.at[r], bit_id(0)
        )

    def shard_send(k, c):
        return remote(
            sends[k - 1].at[c], recvs[k - 1].at[c], rs_s.at[k - 1, c], rs_r.at[k - 1, c], bit_id(k)
        )

    def gain_send(b):
        device = bit_id(b) if b < bits else peer_id()
        return remote(gp.at[b], gpr.at[b], gg_s.at[b], gg_r.at[b], device)

    ctx_copy().start()

    @pl.loop(0, half)
    def _(c):
        w_copy(half + c).start()

    @pl.loop(0, half)
    def _(c):
        w_copy(c).start()
        cot_copy(c).start()

    gain_copy().start()

    @pl.loop(0, chunks)
    def _(r):
        for copy in m_copies(r):
            copy.start()

    barrier = pltpu.get_barrier_semaphore()
    pl.semaphore_signal(barrier, inc=1, device_id=peer_id(), device_id_type=MESH)
    for bit in range(bits):
        pl.semaphore_signal(barrier, inc=1, device_id=bit_id(bit), device_id_type=MESH)
    pl.semaphore_wait(barrier, bits + 1)

    ctx_copy().wait()
    ctx_send().start()

    @pl.loop(0, half)
    def _(c):
        w_copy(half + c).wait()
        psend[c] = jnp.dot(
            ctx[0:tok], wv[half + c], preferred_element_type=F32
        ).astype(BF16)
        partial_send(c).start()

    @pl.loop(0, half)
    def _(c):
        w_copy(c).wait()
        own[c] = jnp.dot(ctx[0:tok], wv[c], preferred_element_type=F32)
        cot_copy(c).wait()

    gain_copy().wait()

    ctx_send().wait_recv()
    ctxt_all[...] = jnp.transpose(ctx[...].astype(F32)).reshape(n, rows, 2 * tok)
    blocks = []
    for place in range(n // 2):
        shard = dp
        for k in range(1, bits):
            if not (place >> (bits - 1 - k)) & 1:
                shard = flip(shard, k)
        blocks.append(ctxt_all[shard])
    ctxt[...] = jnp.concatenate(blocks, axis=0).astype(BF16)

    def fold(value):
        total = value[:, 0:128]
        for lane in range(128, cw, 128):
            total = total + value[:, lane:lane + 128]
        return total

    def gather_stats(c, carry):
        square, cross = carry
        partial_send(c).wait_recv()
        attn = own[c] + precv[c].astype(F32)
        own[c] = attn
        scaled = cot[c].astype(F32) * gain[c]
        return square + fold(attn * attn), cross + fold(scaled * attn)

    zero = jnp.zeros((tok, 128), F32)
    square, cross = lax.fori_loop(0, half, gather_stats, (zero, zero))
    square = jnp.sum(square, axis=1, keepdims=True)
    cross = jnp.sum(cross, axis=1, keepdims=True)
    even = lax.broadcasted_iota(jnp.int32, (tok, 128), 1) % 2 == 0
    stat_s[...] = jnp.transpose(jnp.where(even, square, cross))[0:8]
    stat_send().start()
    stat_send().wait_recv()
    totals = jnp.transpose(jnp.concatenate([stat_s[...] + stat_r[...]] * 16, axis=0))
    inverse = lax.rsqrt(totals[:, 0:1] / width + norm_floor)
    shift = inverse * totals[:, 1:2] / width

    @pl.loop(0, half)
    def _(c):
        upstream = cot[c].astype(F32)
        normed = own[c] * inverse
        g[c, 0:tok] = (inverse * (upstream * gain[c] - normed * shift)).astype(BF16)
        grad_peer(c).start()
        grad_mate(c).start()
        gp[0, c] = jnp.sum(upstream * normed, axis=0, keepdims=True)

    gc_acc[...] = jnp.zeros_like(gc_acc)
    gain_send(0).start()

    n_final = chunks + LAG * (bits - 1)

    @pl.loop(0, max(n_final, bits + 3))
    def _(t):
        ahead = t + 1

        @pl.when((ahead >= half) & (ahead < chunks))
        def _():
            grad_peer(ahead - half).wait_recv()
            grad_mate(ahead).start()

        @pl.when(t < chunks)
        def _():
            grad_mate(t).wait_recv()
            product = jnp.dot(ctxt[...], g[t], preferred_element_type=F32)
            cut = product.shape[0] // 2
            sends[0][t] = product[:cut].astype(BF16)
            shard_send(1, t).start()
            keeps[0][t] = product[cut:]
            gc_acc[...] += lax.dot_general(
                g[t, 0:tok], wv[t], (((1,), (1,)), ((), ())), preferred_element_type=F32
            )

        @pl.when(t == chunks)
        def _():
            gc_out[...] = gc_acc[...].astype(BF16)
            pltpu.make_async_copy(gc_out, gc_hbm, gc_sem).start()

        for b in range(bits + 1):
            @pl.when(t == b + 1)
            def _():
                gain_send(b).wait_recv()
                if b < bits:
                    gp[b + 1] = gp[b] + gpr[b]
                    gain_send(b + 1).start()
                else:
                    gfin[pl.ds(mp * half, half)] = gp[bits]
                    gfin[pl.ds(peer * half, half)] = gpr[bits]
                    pltpu.make_async_copy(gfin, gg_hbm, gg_sem).start()

        for k in range(bits - 1, 0, -1):
            c = t - LAG * k

            @pl.when((c >= 0) & (c < chunks))
            def _():
                shard_send(k, c).wait_recv()
                total = keeps[k - 1][c] + recvs[k - 1][c].astype(F32)
                if k < bits - 1:
                    cut = total.shape[0] // 2
                    sends[k][c] = total[:cut].astype(BF16)
                    shard_send(k + 1, c).start()
                    keeps[k][c] = total[cut:]
                else:
                    for copy in m_copies(c):
                        copy.wait()
                    first = beta_one * m1[c] + (1.0 - beta_one) * total
                    second = beta_two * m2[c] + (1.0 - beta_two) * total * total
                    nw[c] = (
                        master[c].astype(F32) - learn_rate * first / (jnp.sqrt(second) + adam_floor)
                    ).astype(BF16)
                    m1[c] = first
                    m2[c] = second
                    for copy in out_copies(c):
                        copy.start()

    ctx_send().wait_send()
    stat_send().wait_send()

    @pl.loop(0, half)
    def _(c):
        partial_send(c).wait_send()
        grad_peer(c).wait_send()

    for b in range(bits + 1):
        gain_send(b).wait_send()

    @pl.loop(0, chunks)
    def _(r):
        grad_mate(r).wait_send()
        for k in range(1, bits):
            shard_send(k, r).wait_send()
        for copy in out_copies(r):
            copy.wait()

    pltpu.make_async_copy(gc_out, gc_hbm, gc_sem).wait()
    pltpu.make_async_copy(gfin, gg_hbm, gg_sem).wait()


def per_device(n, context, out_weight, cotangent, norm_gain, first_moment, second_moment):
    tok, heads = context.shape
    width = out_weight.shape[1]
    rows = first_moment.shape[1]
    bits = n.bit_length() - 1
    cw = 256
    half = width // (2 * cw)
    chunks = 2 * half
    cfg = (n, bits, half, chunks, cw, rows, tok, heads, width)
    sizes = [(n >> (k + 1)) * rows for k in range(1, bits)]
    dma = pltpu.SemaphoreType.DMA
    vmem = pltpu.VMEM
    scratch = [
        vmem((chunks, heads, cw), BF16),
        vmem((2 * tok, heads), BF16),
        vmem((n, rows, 2 * tok), F32),
        vmem((heads // 2, 2 * tok), BF16),
        vmem((half, tok, cw), BF16),
        vmem((half, 1, cw), F32),
        vmem((half, tok, cw), BF16),
        vmem((half, tok, cw), BF16),
        vmem((half, tok, cw), F32),
        vmem((8, tok), F32),
        vmem((8, tok), F32),
        vmem((chunks, 2 * tok, cw), BF16),
        tuple(vmem((chunks, size, cw), BF16) for size in sizes),
        tuple(vmem((chunks, size, cw), BF16) for size in sizes),
        tuple(vmem((chunks, size, cw), F32) for size in sizes),
        vmem((chunks, rows, cw), F32),
        vmem((chunks, rows, cw), F32),
        vmem((chunks, rows, cw), BF16),
        vmem((chunks, rows, cw), BF16),
        vmem((tok, heads), F32),
        vmem((tok, heads), BF16),
        vmem((bits + 1, half, 1, cw), F32),
        vmem((bits + 1, half, 1, cw), F32),
        vmem((chunks, 1, cw), F32),
        dma((2,)), dma((chunks,)), dma((half,)), dma((3, chunks)), dma((3, chunks)), dma, dma,
        dma((half,)), dma((half,)), dma, dma, dma, dma,
        dma((half,)), dma((half,)), dma((chunks,)), dma((chunks,)),
        dma((bits - 1, chunks)), dma((bits - 1, chunks)), dma((bits + 1,)), dma((bits + 1,)),
    ]
    anywhere = pl.BlockSpec(memory_space=pl.ANY)
    new_weight, new_first, new_second, grad_gain, grad_context = pl.pallas_call(
        functools.partial(kernel, cfg),
        out_shape=(
            jax.ShapeDtypeStruct(first_moment.shape, BF16),
            jax.ShapeDtypeStruct(first_moment.shape, F32),
            jax.ShapeDtypeStruct(first_moment.shape, F32),
            jax.ShapeDtypeStruct((chunks, 1, cw), F32),
            jax.ShapeDtypeStruct((tok, heads), BF16),
        ),
        in_specs=[anywhere] * 6,
        out_specs=(anywhere,) * 5,
        scratch_shapes=scratch,
        compiler_params=pltpu.CompilerParams(
            collective_id=0, has_side_effects=True, vmem_limit_bytes=60 * 1024 * 1024
        ),
    )(context, out_weight, cotangent, norm_gain.reshape(chunks, 1, cw), first_moment, second_moment)
    return (new_weight, new_first, new_second, grad_gain.reshape(width), grad_context)


def solution(mesh):
    return jax.shard_map(
        functools.partial(per_device, mesh.shape["dp"]),
        mesh=mesh,
        in_specs=(
            P("dp", "mp"),
            P("mp", None),
            P("dp", None),
            P(),
            P("mp", "dp", None),
            P("mp", "dp", None),
        ),
        out_specs=(
            P("mp", "dp", None),
            P("mp", "dp", None),
            P("mp", "dp", None),
            P(),
            P("dp", "mp"),
        ),
        check_vma=False,
    )
```

time: 324 us -> 106 us (0.33)
  waiting for transfers between devices: 194 us -> 0 us
  Pallas kernels: 0 us -> 94.6 us
  blocking collectives: 47.8 us -> 0 us
  matrix products: 23.9 us -> 0 us
  local copies, waits for them, and re-layouts: 31.5 us -> 10.1 us
  between operations: 13.8 us -> 0.64 us
  other arithmetic: 11.9 us -> 0.75 us
    unnamed x4 -> x0, waiting for transfers between devices: 98.2 us -> none
    pallas_call x0 -> x1, Pallas kernels: none -> 94.6 us  [per_device(): pl.pallas_call(functools.partial(kernel, cfg), out_shape=(jax.ShapeDtypeS...]
    reduce_scatter x1 -> x0, waiting for transfers between devices: 60.8 us -> none  [per_device(): lax.psum_scatter(partial_value, 'mp', scatter_dimension=1, tiled=True)]
    psum x3 -> x0, blocking collectives: 43.5 us -> none  [the longest x1 33.6 us: per_device(): gain_total = lax.psum(gain_part, 'dp')]
    all_gather x1 -> x0, waiting for transfers between devices: 35.4 us -> none  [per_device(): grad_attn = lax.all_gather(grad_half, 'mp', axis=1, tiled=True)]
    dot_general x3 -> x0, matrix products: 23.9 us -> none  [the longest x1 8.95 us: per_device(): lax.dot_general(context, grad_attn, (((0,), (0,)), ((), ())), preferred_e...]
    unnamed x22 -> x4, local copies, waits for them, and re-layouts: 30.3 us -> 8.11 us
    convert_element_type x2 -> x0, other arithmetic: 7.73 us -> none  [the longest x1 4.92 us: adam_update(): (master - learn_rate * new_first / (jnp.sqrt(new_second) + adam_floor)).a...]
  transfers between devices with their start and end apart: 3 -> 0, of which waited for: 3 -> 0; matrix products, arithmetic and copies ran while one was open for 4% -> 0% of each run, Pallas kernels for 0% -> 0%
where the time goes in v1:
time: 106 us
  Pallas kernels  94.6 us (89%)
  local copies, waits for them, and re-layouts  10.1 us (10%)
    pallas_call x1, Pallas kernels, per_device(): pl.pallas_call(functools.partial(kernel, cfg), out_shape=(jax.ShapeDtypeS...  94.6 us
    unnamed x4, local copies, waits for them, and re-layouts  8.11 us

profile of v1, /device:TPU:0, one launch (start us, length us, event | category | flops | bytes accessed | tf_op | source)
XLA Modules:
  0.0 106.1 jit_solution(10973648828819526000)
XLA Ops:
  0.6 1.3 %reshape.16.gain_hbm = f32[14,1,256]{2,1,0:T(1,128)} reshape(f32[3584]{0:T(1024)} %param.9) | data formatting | bytes 28672 | tf_op jit(solution)/shard_map/reshape | solution.py:352
  2.0 94.6 %shard_map.101 = (bf16[1,64,3584]{2,1,0:T(8,128)(2,1)}, f32[1,64,3584]{2,1,0:T(8,128)}, f32[1,64,3584]{2,1,0:T(8,128)}, f32[14,1,256]{2,1,0:T(1,128)}, bf16[320,1024]{1,0:T(8,128)(2,1)}) custom-call(bf16[320,1024]{1,0:T(8,128)(2,1)} %ctx_hbm.1, bf16[1024,3584]{1,0:T(8,128)(2,1)} %w_hbm.1, bf16[320,3584]{1,0:T(8,128)(2,1)} %cot_hbm.1, ...), custom_call_target="tpu_custom_call" | custom-call | tf_op jit(solution)/shard_map/pallas_call | solution.py:337
  96.6 0.8 reduce
  97.4 0.6 reshape.17
  98.0 1.8 %copy.15 = bf16[1,64,3584]{2,1,0:T(8,128)(2,1)} copy(bf16[1,64,3584]{2,1,0:T(8,128)(2,1)} %get-tuple-element.20) | data formatting | bytes 917504
  99.8 2.2 %copy.16 = f32[1,64,3584]{2,1,0:T(8,128)} copy(f32[1,64,3584]{2,1,0:T(8,128)} %get-tuple-element.21) | data formatting | bytes 1835008
  101.9 2.2 %copy.17 = f32[1,64,3584]{2,1,0:T(8,128)} copy(f32[1,64,3584]{2,1,0:T(8,128)} %get-tuple-element.22) | data formatting | bytes 1835008
  104.1 2.0 %copy.18 = bf16[320,1024]{1,0:T(8,128)(2,1)} copy(bf16[320,1024]{1,0:T(8,128)(2,1)} %get-tuple-element.24) | data formatting | bytes 1310720

commit v2 on v1

--- a/solution.py
+++ b/solution.py
@@ -22,11 +22,11 @@
 def kernel(
     cfg,
     ctx_hbm, w_hbm, cot_hbm, gain_hbm, m1_hbm, m2_hbm,
-    nw_hbm, n1_hbm, n2_hbm, gg_hbm, gc_hbm,
-    wv, ctx, ctxt_all, ctxt, cot, gain, psend, precv, own, stat_s, stat_r, g,
-    sends, recvs, keeps, m1, m2, master, nw, gc_acc, gc_out,
-    gp, gpr, gfin,
-    in_sem, w_sem, cot_sem, m_sem, out_sem, gc_sem, gg_sem,
+    nw, n1, n2, gfin, gc_out,
+    wv, ctx, ctxt_all, ctxt, cot, gain_flat, gain, psend, precv, own, stat_s, stat_r, g,
+    sends, recvs, keeps, m1, m2, master, gc_acc,
+    gp, gpr,
+    in_sem, w_sem, cot_sem, m_sem,
     ps_s, ps_r, st_s, st_r, cx_s, cx_r, gy_s, gy_r, gm_s, gm_r,
     rs_s, rs_r, gg_s, gg_r,
 ):
@@ -43,6 +43,16 @@
     def bit_id(bit):
         return (flip(dp, bit), mp)
 
+    def late(c):
+        return c % half == half // 2
+
+    def turn_bits(k):
+        return k, k + 1 if k < bits - 1 else 1
+
+    def turn_id(k, c):
+        usual, other = turn_bits(k)
+        return (jnp.where(late(c), flip(dp, other), flip(dp, usual)), mp)
+
     def column(r):
         first = jnp.where(r < half, mp * half + r, peer * half + r - half)
         return pl.multiple_of(first * cw, cw)
@@ -51,7 +61,7 @@
         return pltpu.make_async_copy(ctx_hbm, ctx.at[pl.ds(0, tok)], in_sem.at[0])
 
     def gain_copy():
-        return pltpu.make_async_copy(gain_hbm.at[pl.ds(mp * half, half)], gain, in_sem.at[1])
+        return pltpu.make_async_copy(gain_hbm, gain_flat, in_sem.at[1])
 
     def w_copy(r):
         return pltpu.make_async_copy(w_hbm.at[:, pl.ds(column(r), cw)], wv.at[r], w_sem.at[r])
@@ -69,14 +79,6 @@
             ),
         )
 
-    def out_copies(r):
-        cols = pl.ds(column(r), cw)
-        return (
-            pltpu.make_async_copy(nw.at[r], nw_hbm.at[0, :, cols], out_sem.at[0, r]),
-            pltpu.make_async_copy(m1.at[r], n1_hbm.at[0, :, cols], out_sem.at[1, r]),
-            pltpu.make_async_copy(m2.at[r], n2_hbm.at[0, :, cols], out_sem.at[2, r]),
-        )
-
     def remote(src, dst, send_sem, recv_sem, device):
         return pltpu.make_async_remote_copy(
             src_ref=src, dst_ref=dst, send_sem=send_sem, recv_sem=recv_sem,
@@ -104,7 +106,7 @@
 
     def shard_send(k, c):
         return remote(
-            sends[k - 1].at[c], recvs[k - 1].at[c], rs_s.at[k - 1, c], rs_r.at[k - 1, c], bit_id(k)
+            sends[k - 1].at[c], recvs[k - 1].at[c], rs_s.at[k - 1, c], rs_r.at[k - 1, c], turn_id(k, c)
         )
 
     def gain_send(b):
@@ -153,17 +155,20 @@
         cot_copy(c).wait()
 
     gain_copy().wait()
+    for r in range(chunks):
+        gain[r] = gain_flat[r * cw:(r + 1) * cw].reshape(1, cw)
 
     ctx_send().wait_recv()
     ctxt_all[...] = jnp.transpose(ctx[...].astype(F32)).reshape(n, rows, 2 * tok)
-    blocks = []
-    for place in range(n // 2):
-        shard = dp
-        for k in range(1, bits):
-            if not (place >> (bits - 1 - k)) & 1:
-                shard = flip(shard, k)
-        blocks.append(ctxt_all[shard])
-    ctxt[...] = jnp.concatenate(blocks, axis=0).astype(BF16)
+    for order in range(2):
+        blocks = []
+        for place in range(n // 2):
+            shard = dp
+            for k in range(1, bits):
+                if not (place >> (bits - 1 - k)) & 1:
+                    shard = flip(shard, turn_bits(k)[order])
+            blocks.append(ctxt_all[shard])
+        ctxt[order] = jnp.concatenate(blocks, axis=0).astype(BF16)
 
     def fold(value):
         total = value[:, 0:128]
@@ -176,7 +181,7 @@
         partial_send(c).wait_recv()
         attn = own[c] + precv[c].astype(F32)
         own[c] = attn
-        scaled = cot[c].astype(F32) * gain[c]
+        scaled = cot[c].astype(F32) * gain[mp * half + c]
         return square + fold(attn * attn), cross + fold(scaled * attn)
 
     zero = jnp.zeros((tok, 128), F32)
@@ -195,7 +200,7 @@
     def _(c):
         upstream = cot[c].astype(F32)
         normed = own[c] * inverse
-        g[c, 0:tok] = (inverse * (upstream * gain[c] - normed * shift)).astype(BF16)
+        g[c, 0:tok] = (inverse * (upstream * gain[mp * half + c] - normed * shift)).astype(BF16)
         grad_peer(c).start()
         grad_mate(c).start()
         gp[0, c] = jnp.sum(upstream * normed, axis=0, keepdims=True)
@@ -217,7 +222,7 @@
         @pl.when(t < chunks)
         def _():
             grad_mate(t).wait_recv()
-            product = jnp.dot(ctxt[...], g[t], preferred_element_type=F32)
+            product = jnp.dot(ctxt[late(t).astype(jnp.int32)], g[t], preferred_element_type=F32)
             cut = product.shape[0] // 2
             sends[0][t] = product[:cut].astype(BF16)
             shard_send(1, t).start()
@@ -229,7 +234,6 @@
         @pl.when(t == chunks)
         def _():
             gc_out[...] = gc_acc[...].astype(BF16)
-            pltpu.make_async_copy(gc_out, gc_hbm, gc_sem).start()
 
         for b in range(bits + 1):
             @pl.when(t == b + 1)
@@ -241,7 +245,6 @@
                 else:
                     gfin[pl.ds(mp * half, half)] = gp[bits]
                     gfin[pl.ds(peer * half, half)] = gpr[bits]
-                    pltpu.make_async_copy(gfin, gg_hbm, gg_sem).start()
 
         for k in range(bits - 1, 0, -1):
             c = t - LAG * k
@@ -260,13 +263,12 @@
                         copy.wait()
                     first = beta_one * m1[c] + (1.0 - beta_one) * total
                     second = beta_two * m2[c] + (1.0 - beta_two) * total * total
-                    nw[c] = (
+                    cols = pl.ds(column(c), cw)
+                    nw[0, :, cols] = (
                         master[c].astype(F32) - learn_rate * first / (jnp.sqrt(second) + adam_floor)
                     ).astype(BF16)
-                    m1[c] = first
-                    m2[c] = second
-                    for copy in out_copies(c):
-                        copy.start()
+                    n1[0, :, cols] = first
+                    n2[0, :, cols] = second
 
     ctx_send().wait_send()
     stat_send().wait_send()
@@ -284,11 +286,20 @@
         grad_mate(r).wait_send()
         for k in range(1, bits):
             shard_send(k, r).wait_send()
-        for copy in out_copies(r):
-            copy.wait()
-
-    pltpu.make_async_copy(gc_out, gc_hbm, gc_sem).wait()
-    pltpu.make_async_copy(gfin, gg_hbm, gg_sem).wait()
+
+
+def settle(nw, n1, n2, gg, gc, nw_out, n1_out, n2_out, gg_out, gc_out, flat, sem):
+    pairs = ((nw, nw_out), (n1, n1_out), (n2, n2_out), (gc, gc_out))
+    copies = [pltpu.make_async_copy(a, b, sem.at[i]) for i, (a, b) in enumerate(pairs)]
+    for copy in copies:
+        copy.start()
+    chunks, _, cw = gg.shape
+    for r in range(chunks):
+        flat[r * cw:(r + 1) * cw] = gg[r].reshape(cw)
+    copies.append(pltpu.make_async_copy(flat, gg_out, sem.at[4]))
+    copies[-1].start()
+    for copy in copies:
+        copy.wait()
 
 
 def per_device(n, context, out_weight, cotangent, norm_gain, first_moment, second_moment):
@@ -307,9 +318,10 @@
         vmem((chunks, heads, cw), BF16),
         vmem((2 * tok, heads), BF16),
         vmem((n, rows, 2 * tok), F32),
-        vmem((heads // 2, 2 * tok), BF16),
+        vmem((2, heads // 2, 2 * tok), BF16),
         vmem((half, tok, cw), BF16),
-        vmem((half, 1, cw), F32),
+        vmem((width,), F32),
+        vmem((chunks, 1, cw), F32),
         vmem((half, tok, cw), BF16),
         vmem((half, tok, cw), BF16),
         vmem((half, tok, cw), F32),
@@ -322,18 +334,15 @@
         vmem((chunks, rows, cw), F32),
         vmem((chunks, rows, cw), F32),
         vmem((chunks, rows, cw), BF16),
-        vmem((chunks, rows, cw), BF16),
         vmem((tok, heads), F32),
-        vmem((tok, heads), BF16),
         vmem((bits + 1, half, 1, cw), F32),
         vmem((bits + 1, half, 1, cw), F32),
-        vmem((chunks, 1, cw), F32),
-        dma((2,)), dma((chunks,)), dma((half,)), dma((3, chunks)), dma((3, chunks)), dma, dma,
+        dma((2,)), dma((chunks,)), dma((half,)), dma((3, chunks)),
         dma((half,)), dma((half,)), dma, dma, dma, dma,
         dma((half,)), dma((half,)), dma((chunks,)), dma((chunks,)),
         dma((bits - 1, chunks)), dma((bits - 1, chunks)), dma((bits + 1,)), dma((bits + 1,)),
     ]
-    anywhere = pl.BlockSpec(memory_space=pl.ANY)
+    anywhere = pl.BlockSpec(memory_space=pltpu.HBM)
     new_weight, new_first, new_second, grad_gain, grad_context = pl.pallas_call(
         functools.partial(kernel, cfg),
         out_shape=(
@@ -344,13 +353,26 @@
             jax.ShapeDtypeStruct((tok, heads), BF16),
         ),
         in_specs=[anywhere] * 6,
-        out_specs=(anywhere,) * 5,
+        out_specs=(pl.BlockSpec(memory_space=pltpu.VMEM),) * 5,
         scratch_shapes=scratch,
         compiler_params=pltpu.CompilerParams(
-            collective_id=0, has_side_effects=True, vmem_limit_bytes=60 * 1024 * 1024
-        ),
-    )(context, out_weight, cotangent, norm_gain.reshape(chunks, 1, cw), first_moment, second_moment)
-    return (new_weight, new_first, new_second, grad_gain.reshape(width), grad_context)
+            collective_id=0, has_side_effects=True, vmem_limit_bytes=50 * 1024 * 1024
+        ),
+    )(context, out_weight, cotangent, norm_gain, first_moment, second_moment)
+    return pl.pallas_call(
+        settle,
+        out_shape=(
+            jax.ShapeDtypeStruct(first_moment.shape, BF16),
+            jax.ShapeDtypeStruct(first_moment.shape, F32),
+            jax.ShapeDtypeStruct(first_moment.shape, F32),
+            jax.ShapeDtypeStruct((width,), F32),
+            jax.ShapeDtypeStruct((tok, heads), BF16),
+        ),
+        in_specs=[pl.BlockSpec(memory_space=pltpu.VMEM)] * 5,
+        out_specs=(anywhere,) * 5,
+        scratch_shapes=[vmem((width,), F32), dma((5,))],
+        compiler_params=pltpu.CompilerParams(vmem_limit_bytes=8 * 1024 * 1024),
+    )(new_weight, new_first, new_second, grad_gain, grad_context)
 
 
 def solution(mesh):

time: 106 us -> 99 us (0.934)
  local copies, waits for them, and re-layouts: 10.1 us -> 1.8 us
  Pallas kernels: 94.6 us -> 96.3 us
    unnamed x4, local copies, waits for them, and re-layouts: 8.11 us -> 1.8 us
    reshape x2 -> x0, local copies, waits for them, and re-layouts: 1.94 us -> none  [the longest x1 1.33 us: per_device(): norm_gain.reshape(chunks, 1, cw)]
    pallas_call x0 -> x1, Pallas kernels: none -> 1.64 us  [per_device(): pl.pallas_call(settle, out_shape=(jax.ShapeDtypeStruct(first_moment.shape...]
where the time goes in v2:
time: 99 us; the launch traced here: 98.7 us
  Pallas kernels  96.3 us (97%)
  local copies, waits for them, and re-layouts  1.8 us (2%)
    pallas_call x1, Pallas kernels, per_device(): pl.pallas_call(functools.partial(kernel, cfg), out_shape=(jax.ShapeDtypeS...  94.7 us

profile of v2, /device:TPU:0, one launch (start us, length us, event | category | flops | bytes accessed | tf_op | source)
XLA Modules:
  0.0 98.7 jit_solution(1684237530569139579)
XLA Ops:
  0.6 0.0 copy-start
  0.6 1.1 %copy-done = bf16[320,1024]{1,0:T(8,128)(2,1)S(1)} copy-done((bf16[320,1024]{1,0:T(8,128)(2,1)S(1)}, bf16[320,1024]{1,0:T(8,128)(2,1)}, u32[]{:S(2)}) %copy-start) | copy-done | bytes 655384
  1.7 0.0 copy-start.1
  1.7 0.7 copy-done.1
  2.4 94.7 %shard_map.101 = (bf16[1,64,3584]{2,1,0:T(8,128)(2,1)S(1)}, f32[1,64,3584]{2,1,0:T(8,128)S(1)}, f32[1,64,3584]{2,1,0:T(8,128)S(1)}, f32[14,1,256]{2,1,0:T(1,128)S(1)}, bf16[320,1024]{1,0:T(8,128)(2,1)S(1)}) custom-call(bf16[320,1024]{1,0:T(8,128)(2,1)S(1)} %copy-done, bf16[1024,3584]{1,0:T(8,128)(2,1)} %w_hbm.1, bf16[320,3584]{1,0:T(8,128)(2,1)} %cot_hbm.1, ...), custom_call_target="tpu_custom_call" | custom-call | tf_op jit(solution)/shard_map/pallas_call | solution.py:346
  97.1 1.6 %shard_map.102 = (bf16[1,64,3584]{2,1,0:T(8,128)(2,1)}, f32[1,64,3584]{2,1,0:T(8,128)}, f32[1,64,3584]{2,1,0:T(8,128)}, f32[3584]{0:T(1024)}, bf16[320,1024]{1,0:T(8,128)(2,1)}) custom-call(bf16[1,64,3584]{2,1,0:T(8,128)(2,1)S(1)} %get-tuple-element.10.nw, f32[1,64,3584]{2,1,0:T(8,128)S(1)} %get-tuple-element.11.n1, ...), custom_call_target="tpu_custom_call" | custom-call | tf_op jit(solution)/shard_map/pallas_call | solution.py:362
Async XLA Ops:
  0.6 1.1 %copy-start = (bf16[320,1024]{1,0:T(8,128)(2,1)S(1)}, bf16[320,1024]{1,0:T(8,128)(2,1)}, u32[]{:S(2)}) copy-start(bf16[320,1024]{1,0:T(8,128)(2,1)} %ctx_hbm.1) | copy-start | bytes 1966084
  1.7 0.7 copy-start.1

commit v3 on v2

--- a/solution.py
+++ b/solution.py
@@ -17,6 +17,7 @@
 F32 = jnp.float32
 BF16 = jnp.bfloat16
 LAG = 2
+AHEAD = 2
 
 
 def kernel(
@@ -43,16 +44,6 @@
     def bit_id(bit):
         return (flip(dp, bit), mp)
 
-    def late(c):
-        return c % half == half // 2
-
-    def turn_bits(k):
-        return k, k + 1 if k < bits - 1 else 1
-
-    def turn_id(k, c):
-        usual, other = turn_bits(k)
-        return (jnp.where(late(c), flip(dp, other), flip(dp, usual)), mp)
-
     def column(r):
         first = jnp.where(r < half, mp * half + r, peer * half + r - half)
         return pl.multiple_of(first * cw, cw)
@@ -106,7 +97,7 @@
 
     def shard_send(k, c):
         return remote(
-            sends[k - 1].at[c], recvs[k - 1].at[c], rs_s.at[k - 1, c], rs_r.at[k - 1, c], turn_id(k, c)
+            sends[k - 1].at[c], recvs[k - 1].at[c], rs_s.at[k - 1, c], rs_r.at[k - 1, c], bit_id(k)
         )
 
     def gain_send(b):
@@ -160,15 +151,14 @@
 
     ctx_send().wait_recv()
     ctxt_all[...] = jnp.transpose(ctx[...].astype(F32)).reshape(n, rows, 2 * tok)
-    for order in range(2):
-        blocks = []
-        for place in range(n // 2):
-            shard = dp
-            for k in range(1, bits):
-                if not (place >> (bits - 1 - k)) & 1:
-                    shard = flip(shard, turn_bits(k)[order])
-            blocks.append(ctxt_all[shard])
-        ctxt[order] = jnp.concatenate(blocks, axis=0).astype(BF16)
+    blocks = []
+    for place in range(n // 2):
+        shard = dp
+        for k in range(1, bits):
+            if not (place >> (bits - 1 - k)) & 1:
+                shard = flip(shard, k)
+        blocks.append(ctxt_all[shard])
+    ctxt[...] = jnp.concatenate(blocks, axis=0).astype(BF16)
 
     def fold(value):
         total = value[:, 0:128]
@@ -212,7 +202,7 @@
 
     @pl.loop(0, max(n_final, bits + 3))
     def _(t):
-        ahead = t + 1
+        ahead = t + AHEAD
 
         @pl.when((ahead >= half) & (ahead < chunks))
         def _():
@@ -222,7 +212,7 @@
         @pl.when(t < chunks)
         def _():
             grad_mate(t).wait_recv()
-            product = jnp.dot(ctxt[late(t).astype(jnp.int32)], g[t], preferred_element_type=F32)
+            product = jnp.dot(ctxt[...], g[t], preferred_element_type=F32)
             cut = product.shape[0] // 2
             sends[0][t] = product[:cut].astype(BF16)
             shard_send(1, t).start()
@@ -318,7 +308,7 @@
         vmem((chunks, heads, cw), BF16),
         vmem((2 * tok, heads), BF16),
         vmem((n, rows, 2 * tok), F32),
-        vmem((2, heads // 2, 2 * tok), BF16),
+        vmem((heads // 2, 2 * tok), BF16),
         vmem((half, tok, cw), BF16),
         vmem((width,), F32),
         vmem((chunks, 1, cw), F32),

time: 99 us -> 96.8 us (0.978)
  Pallas kernels: 96.3 us -> 94.1 us
    pallas_call x1, Pallas kernels: 94.7 us -> 92.5 us  [per_device(): pl.pallas_call(functools.partial(kernel, cfg), out_shape=(jax.ShapeDtypeS...]
where the time goes in v3:
time: 96.8 us; the launch traced here: 96.6 us
  Pallas kernels  94.1 us (97%)
  local copies, waits for them, and re-layouts  1.8 us (2%)
    pallas_call x1, Pallas kernels, per_device(): pl.pallas_call(functools.partial(kernel, cfg), out_shape=(jax.ShapeDtypeS...  92.5 us

profile of v3, /device:TPU:0, one launch (start us, length us, event | category | flops | bytes accessed | tf_op | source)
XLA Modules:
  0.0 96.6 jit_solution(14305384820833555348)
XLA Ops:
  0.6 0.0 copy-start
  0.6 1.1 %copy-done = bf16[320,1024]{1,0:T(8,128)(2,1)S(1)} copy-done((bf16[320,1024]{1,0:T(8,128)(2,1)S(1)}, bf16[320,1024]{1,0:T(8,128)(2,1)}, u32[]{:S(2)}) %copy-start) | copy-done | bytes 655384
  1.7 0.0 copy-start.1
  1.7 0.7 copy-done.1
  2.4 92.5 %shard_map.101 = (bf16[1,64,3584]{2,1,0:T(8,128)(2,1)S(1)}, f32[1,64,3584]{2,1,0:T(8,128)S(1)}, f32[1,64,3584]{2,1,0:T(8,128)S(1)}, f32[14,1,256]{2,1,0:T(1,128)S(1)}, bf16[320,1024]{1,0:T(8,128)(2,1)S(1)}) custom-call(bf16[320,1024]{1,0:T(8,128)(2,1)S(1)} %copy-done, bf16[1024,3584]{1,0:T(8,128)(2,1)} %w_hbm.1, bf16[320,3584]{1,0:T(8,128)(2,1)} %cot_hbm.1, ...), custom_call_target="tpu_custom_call" | custom-call | tf_op jit(solution)/shard_map/pallas_call | solution.py:336
  94.9 1.6 %shard_map.102 = (bf16[1,64,3584]{2,1,0:T(8,128)(2,1)}, f32[1,64,3584]{2,1,0:T(8,128)}, f32[1,64,3584]{2,1,0:T(8,128)}, f32[3584]{0:T(1024)}, bf16[320,1024]{1,0:T(8,128)(2,1)}) custom-call(bf16[1,64,3584]{2,1,0:T(8,128)(2,1)S(1)} %get-tuple-element.10.nw, f32[1,64,3584]{2,1,0:T(8,128)S(1)} %get-tuple-element.11.n1, ...), custom_call_target="tpu_custom_call" | custom-call | tf_op jit(solution)/shard_map/pallas_call | solution.py:352
Async XLA Ops:
  0.6 1.1 %copy-start = (bf16[320,1024]{1,0:T(8,128)(2,1)S(1)}, bf16[320,1024]{1,0:T(8,128)(2,1)}, u32[]{:S(2)}) copy-start(bf16[320,1024]{1,0:T(8,128)(2,1)} %ctx_hbm.1) | copy-start | bytes 1966084
  1.7 0.7 copy-start.1

commit v4 on v3

--- a/solution.py
+++ b/solution.py
@@ -110,18 +110,6 @@
     def _(c):
         w_copy(half + c).start()
 
-    @pl.loop(0, half)
-    def _(c):
-        w_copy(c).start()
-        cot_copy(c).start()
-
-    gain_copy().start()
-
-    @pl.loop(0, chunks)
-    def _(r):
-        for copy in m_copies(r):
-            copy.start()
-
     barrier = pltpu.get_barrier_semaphore()
     pl.semaphore_signal(barrier, inc=1, device_id=peer_id(), device_id_type=MESH)
     for bit in range(bits):
@@ -133,6 +121,13 @@
 
     @pl.loop(0, half)
     def _(c):
+        w_copy(c).start()
+        cot_copy(c).start()
+
+    gain_copy().start()
+
+    @pl.loop(0, half)
+    def _(c):
         w_copy(half + c).wait()
         psend[c] = jnp.dot(
             ctx[0:tok], wv[half + c], preferred_element_type=F32
@@ -144,6 +139,11 @@
         w_copy(c).wait()
         own[c] = jnp.dot(ctx[0:tok], wv[c], preferred_element_type=F32)
         cot_copy(c).wait()
+
+    @pl.loop(0, chunks)
+    def _(r):
+        for copy in m_copies(r):
+            copy.start()
 
     gain_copy().wait()
     for r in range(chunks):

time: 96.8 us -> 96.4 us (level)
  no operation moved by 1% of the time
where the time goes in v4:
time: 96.4 us; the launch traced here: 96.2 us
  Pallas kernels  93.7 us (97%)
  local copies, waits for them, and re-layouts  1.8 us (2%)
    pallas_call x1, Pallas kernels, per_device(): pl.pallas_call(functools.partial(kernel, cfg), out_shape=(jax.ShapeDtypeS...  92.1 us

profile of v4, /device:TPU:0, one launch (start us, length us, event | category | flops | bytes accessed | tf_op | source)
XLA Modules:
  0.0 96.2 jit_solution(6183800590936050956)
XLA Ops:
  0.6 0.0 copy-start
  0.6 1.1 %copy-done = bf16[320,1024]{1,0:T(8,128)(2,1)S(1)} copy-done((bf16[320,1024]{1,0:T(8,128)(2,1)S(1)}, bf16[320,1024]{1,0:T(8,128)(2,1)}, u32[]{:S(2)}) %copy-start) | copy-done | bytes 655384
  1.7 0.0 copy-start.1
  1.7 0.7 copy-done.1
  2.4 92.1 %shard_map.101 = (bf16[1,64,3584]{2,1,0:T(8,128)(2,1)S(1)}, f32[1,64,3584]{2,1,0:T(8,128)S(1)}, f32[1,64,3584]{2,1,0:T(8,128)S(1)}, f32[14,1,256]{2,1,0:T(1,128)S(1)}, bf16[320,1024]{1,0:T(8,128)(2,1)S(1)}) custom-call(bf16[320,1024]{1,0:T(8,128)(2,1)S(1)} %copy-done, bf16[1024,3584]{1,0:T(8,128)(2,1)} %w_hbm.1, bf16[320,3584]{1,0:T(8,128)(2,1)} %cot_hbm.1, ...), custom_call_target="tpu_custom_call" | custom-call | tf_op jit(solution)/shard_map/pallas_call | solution.py:336
  94.5 1.6 %shard_map.102 = (bf16[1,64,3584]{2,1,0:T(8,128)(2,1)}, f32[1,64,3584]{2,1,0:T(8,128)}, f32[1,64,3584]{2,1,0:T(8,128)}, f32[3584]{0:T(1024)}, bf16[320,1024]{1,0:T(8,128)(2,1)}) custom-call(bf16[1,64,3584]{2,1,0:T(8,128)(2,1)S(1)} %get-tuple-element.10.nw, f32[1,64,3584]{2,1,0:T(8,128)S(1)} %get-tuple-element.11.n1, ...), custom_call_target="tpu_custom_call" | custom-call | tf_op jit(solution)/shard_map/pallas_call | solution.py:352
Async XLA Ops:
  0.6 1.1 %copy-start = (bf16[320,1024]{1,0:T(8,128)(2,1)S(1)}, bf16[320,1024]{1,0:T(8,128)(2,1)}, u32[]{:S(2)}) copy-start(bf16[320,1024]{1,0:T(8,128)(2,1)} %ctx_hbm.1) | copy-start | bytes 1966084
  1.7 0.7 copy-start.1
